TPU v7x, 32 devices: a whole 2x2x4 slice. The times are simulated.
32 devices in a mesh: dp: 4 (over y, x), ctx: 4 (over z), tensor: 2 (over core).
Axes of the slice: x: 2, y: 2, z: 4, core: 2. Of those that a mesh axis runs over, the one named last changes fastest.
Arguments:
- block_input: bfloat16 [4, 2048, 1536], P('dp', 'ctx'), may hold values from -6 to 6
- segments: int32 [4, 2048], P('dp'), may hold values from 0 to 31, as said below
- positions: int32 [4, 2048], P('dp', 'ctx'), may hold values from 0 to 1023, as said below
- cotangent: bfloat16 [4, 2048, 1536], P('dp', 'ctx'), may hold values from -6 to 6
- norm1_gain: float32 [1536], replicated, may hold values from 0.1 to 1.9
- w_query: bfloat16 [1536, 1536], P(None, 'tensor'), may hold values from -0.15625 to 0.15625
- w_key: bfloat16 [1536, 768], P(None, 'tensor'), may hold values from -0.15625 to 0.15625
- w_value: bfloat16 [1536, 768], P(None, 'tensor'), may hold values from -0.15625 to 0.15625
- w_out: bfloat16 [1536, 1536], P('tensor'), may hold values from -0.625 to 0.625
- norm2_gain: float32 [1536], replicated, may hold values from 0.1 to 1.9
- w_gate: bfloat16 [1536, 4096], P(None, 'tensor'), may hold values from -0.15625 to 0.15625
- w_up: bfloat16 [1536, 4096], P(None, 'tensor'), may hold values from -0.15625 to 0.15625
- w_down: bfloat16 [4096, 1536], P('tensor'), may hold values from -0.09375 to 0.09375
Outputs:
- block_output: bfloat16 [4, 2048, 1536], P('dp', 'ctx')
- grad_input: bfloat16 [4, 2048, 1536], P('dp', 'ctx')
- grad_norm1: float32 [1536], replicated
- grad_query: float32 [1536, 1536], P(None, 'tensor')
- grad_key: float32 [1536, 768], P(None, 'tensor')
- grad_value: float32 [1536, 768], P(None, 'tensor')
- grad_out: float32 [1536, 1536], P('tensor')
- grad_norm2: float32 [1536], replicated
- grad_gate: float32 [1536, 4096], P(None, 'tensor')
- grad_up: float32 [1536, 4096], P(None, 'tensor')
- grad_down: float32 [4096, 1536], P('tensor')
Inputs may be any that keep to these rules, and one draw needn't show every extreme that they name: `segments`: along each sequence the document numbers start at 0, never fall, rise by at most one at a time and only at multiples of 64 positions; every document spans at most 1024 positions. `positions`: each token's position counted from the start of its document.
All inputs are finite; a program needn't handle non-finite values.
Results may differ from a plain program's by a relative error of at most 0.025.
Values may be sent and summed in bfloat16 or wider, within the bound.
A program may use at most 320 MiB of HBM per device.

v0:
```python
import jax
import jax.numpy as jnp
from jax import lax
from jax.sharding import PartitionSpec as P

HDIM = 96
EPSILON = 1e-05
THETA_BASE = 100000.0
MASKED_SCORE = -1e30


def rotate(tensor_in, where, sign):
    half = tensor_in.shape[-1] // 2
    freqs = THETA_BASE ** (-(jnp.arange(half, dtype=jnp.float32) * 2.0) / tensor_in.shape[-1])
    angles = where.astype(jnp.float32)[..., None] * freqs
    cosine = jnp.cos(angles)[..., None, :]
    sine = sign * jnp.sin(angles)[..., None, :]
    first = tensor_in[..., :half]
    second = tensor_in[..., half:]
    return jnp.concatenate(
        [first * cosine - second * sine, second * cosine + first * sine], axis=-1
    )


def tdot(left, right):
    return lax.dot_general(
        left, right, (((0,), (0,)), ((), ())), preferred_element_type=jnp.float32
    )


def rdot(left, right):
    return lax.dot_general(
        left, right, (((1,), (1,)), ((), ())), preferred_element_type=jnp.float32
    )


def masked_scores(query_rows, kv_rows, seg_query, seg_keys, query_index, heads_kv, scale):
    length = kv_rows.shape[0]
    kv_width = kv_rows.shape[1] // 2
    key_all = kv_rows[:, :kv_width].reshape(length, heads_kv, -1)
    value_all = kv_rows[:, kv_width:].reshape(length, heads_kv, -1)
    raw_scores = (
        jnp.einsum("qkgd,skd->kgqs", query_rows, key_all, preferred_element_type=jnp.float32)
        * scale
    )
    allowed = (seg_query[:, None] == seg_keys[None, :]) & (
        jnp.arange(length, dtype=jnp.int32)[None, :] <= query_index[:, None]
    )
    return (jnp.where(allowed, raw_scores, MASKED_SCORE), key_all, value_all)


def shards(
    block_input,
    segments,
    positions,
    cotangent,
    norm1_gain,
    w_query,
    w_key,
    w_value,
    w_out,
    norm2_gain,
    w_gate,
    w_up,
    w_down,
):
    seq_count, stretch_len, width_all = block_input.shape
    length = segments.shape[1]
    heads_q = w_query.shape[1] // HDIM
    heads_kv = w_key.shape[1] // HDIM
    group = heads_q // heads_kv
    kv_width = w_key.shape[1]
    row_count = seq_count * stretch_len
    scale = HDIM ** (-0.5)
    qblock = min(512, stretch_len)
    nblocks = stretch_len // qblock
    offset = lax.axis_index("ctx") * stretch_len
    inputs = block_input.reshape(row_count, width_all).astype(jnp.float32)
    inv_one = lax.rsqrt(jnp.mean(inputs * inputs, axis=1, keepdims=True) + EPSILON)
    normed1 = (inputs * inv_one * norm1_gain).astype(jnp.bfloat16)
    queries = rotate(
        jnp.dot(normed1, w_query, preferred_element_type=jnp.float32).reshape(
            seq_count, stretch_len, heads_q, HDIM
        ),
        positions,
        1.0,
    ).astype(jnp.bfloat16)
    keys = rotate(
        jnp.dot(normed1, w_key, preferred_element_type=jnp.float32).reshape(
            seq_count, stretch_len, heads_kv, HDIM
        ),
        positions,
        1.0,
    ).astype(jnp.bfloat16)
    values = jnp.dot(normed1, w_value, preferred_element_type=jnp.float32).astype(jnp.bfloat16)
    local_kv = jnp.concatenate(
        [
            keys.reshape(seq_count, stretch_len, kv_width),
            values.reshape(seq_count, stretch_len, kv_width),
        ],
        axis=2,
    )
    whole_kv = lax.all_gather(local_kv, "ctx", axis=1, tiled=True)

    def forward_block(item):
        seq_id = item // nblocks
        start = item % nblocks * qblock
        query_rows = lax.dynamic_index_in_dim(queries, seq_id, 0, keepdims=False).reshape(
            qblock, heads_kv, group, HDIM
        )
        seg_row = lax.dynamic_index_in_dim(segments, seq_id, 0, keepdims=False)
        seg_query = lax.dynamic_slice_in_dim(seg_row, offset + start, qblock, 0)
        query_index = offset + start + jnp.arange(qblock, dtype=jnp.int32)
        kv_rows = lax.dynamic_index_in_dim(whole_kv, seq_id, 0, keepdims=False)
        scores, key_all, value_all = masked_scores(
            query_rows, kv_rows, seg_query, seg_row, query_index, heads_kv, scale
        )
        row_max = jnp.max(scores, axis=-1)
        log_total = row_max + jnp.log(jnp.sum(jnp.exp(scores - row_max[..., None]), axis=-1))
        probs = jnp.exp(scores - log_total[..., None]).astype(jnp.bfloat16)
        block_out = jnp.einsum(
            "kgqs,skd->qkgd", probs, value_all, preferred_element_type=jnp.float32
        )
        return (block_out.reshape(qblock, heads_q * HDIM).astype(jnp.bfloat16), log_total)

    outs_blocks, log_totals = lax.map(
        forward_block, jnp.arange(seq_count * nblocks, dtype=jnp.int32)
    )
    attended = outs_blocks.reshape(row_count, heads_q * HDIM)
    log_totals = log_totals.reshape(seq_count, nblocks, heads_kv, group, qblock)
    attn_branch = lax.psum(
        jnp.dot(attended, w_out, preferred_element_type=jnp.float32).astype(jnp.bfloat16), "tensor"
    ).astype(jnp.float32)
    hidden = inputs + attn_branch
    inv_two = lax.rsqrt(jnp.mean(hidden * hidden, axis=1, keepdims=True) + EPSILON)
    normed2 = (hidden * inv_two * norm2_gain).astype(jnp.bfloat16)
    gate = jnp.dot(normed2, w_gate, preferred_element_type=jnp.float32)
    upper = jnp.dot(normed2, w_up, preferred_element_type=jnp.float32)
    sigmoid_gate = jax.nn.sigmoid(gate)
    activated = gate * sigmoid_gate
    mixed = (activated * upper).astype(jnp.bfloat16)
    ffn_branch = lax.psum(
        jnp.dot(mixed, w_down, preferred_element_type=jnp.float32).astype(jnp.bfloat16), "tensor"
    ).astype(jnp.float32)
    block_output = (
        (hidden + ffn_branch).astype(jnp.bfloat16).reshape(seq_count, stretch_len, width_all)
    )
    grad_rows_out = cotangent.reshape(row_count, width_all)
    grad_wdown = tdot(mixed, grad_rows_out)
    grad_mixed = rdot(grad_rows_out, w_down)
    grad_gate_act = (
        grad_mixed * upper * sigmoid_gate * (1.0 + gate * (1.0 - sigmoid_gate))
    ).astype(jnp.bfloat16)
    grad_upper = (grad_mixed * activated).astype(jnp.bfloat16)
    grad_wgate = tdot(normed2, grad_gate_act)
    grad_wup = tdot(normed2, grad_upper)
    grad_normed2 = lax.psum(
        (rdot(grad_gate_act, w_gate) + rdot(grad_upper, w_up)).astype(jnp.bfloat16), "tensor"
    ).astype(jnp.float32)
    scaled_two = grad_normed2 * norm2_gain
    grad_gain_two = jnp.sum(grad_normed2 * hidden * inv_two, axis=0)
    grad_hidden = (
        grad_rows_out.astype(jnp.float32)
        + inv_two * scaled_two
        - hidden
        * (inv_two * inv_two * inv_two)
        * jnp.mean(scaled_two * hidden, axis=1, keepdims=True)
    )
    grad_branch = grad_hidden.astype(jnp.bfloat16)
    grad_wout = tdot(attended, grad_branch)
    grad_attended = rdot(grad_branch, w_out).astype(jnp.bfloat16)
    attended_seq = attended.reshape(seq_count, stretch_len, heads_q * HDIM)
    grad_att_seq = grad_attended.reshape(seq_count, stretch_len, heads_q * HDIM)

    def backward_seq(seq_id):
        kv_rows = lax.dynamic_index_in_dim(whole_kv, seq_id, 0, keepdims=False)
        seg_row = lax.dynamic_index_in_dim(segments, seq_id, 0, keepdims=False)
        query_seq = lax.dynamic_index_in_dim(queries, seq_id, 0, keepdims=False)
        out_seq = lax.dynamic_index_in_dim(attended_seq, seq_id, 0, keepdims=False)
        grad_seq = lax.dynamic_index_in_dim(grad_att_seq, seq_id, 0, keepdims=False)
        log_seq = lax.dynamic_index_in_dim(log_totals, seq_id, 0, keepdims=False)

        def backward_block(carry, block_id):
            start = block_id * qblock
            query_rows = query_seq.reshape(qblock, heads_kv, group, HDIM)
            out_rows = out_seq.reshape(qblock, heads_kv, group, HDIM)
            grad_rows = grad_seq.reshape(qblock, heads_kv, group, HDIM)
            seg_query = lax.dynamic_slice_in_dim(seg_row, offset + start, qblock, 0)
            query_index = offset + start + jnp.arange(qblock, dtype=jnp.int32)
            scores, key_all, value_all = masked_scores(
                query_rows, kv_rows, seg_query, seg_row, query_index, heads_kv, scale
            )
            log_total = lax.dynamic_index_in_dim(log_seq, block_id, 0, keepdims=False)
            probs = jnp.exp(scores - log_total[..., None])
            probs_half = probs.astype(jnp.bfloat16)
            delta = jnp.sum(
                grad_rows.astype(jnp.float32) * out_rows.astype(jnp.float32), axis=3
            ).transpose(1, 2, 0)
            grad_probs = jnp.einsum(
                "qkgd,skd->kgqs", grad_rows, value_all, preferred_element_type=jnp.float32
            )
            grad_scores = (probs * (grad_probs - delta[..., None])).astype(jnp.bfloat16)
            grad_q = (
                jnp.einsum(
                    "kgqs,skd->qkgd", grad_scores, key_all, preferred_element_type=jnp.float32
                )
                * scale
            )
            grad_k = (
                jnp.einsum(
                    "kgqs,qkgd->skd", grad_scores, query_rows, preferred_element_type=jnp.float32
                )
                * scale
            )
            grad_v = jnp.einsum(
                "kgqs,qkgd->skd", probs_half, grad_rows, preferred_element_type=jnp.float32
            )
            added = jnp.concatenate(
                [grad_k.reshape(length, kv_width), grad_v.reshape(length, kv_width)], axis=1
            )
            return (carry + added, grad_q.reshape(qblock, heads_q * HDIM))

        kv_total, grad_q_blocks = lax.scan(
            backward_block,
            jnp.zeros((length, 2 * kv_width), jnp.float32),
            jnp.arange(nblocks, dtype=jnp.int32),
        )
        return (grad_q_blocks.reshape(stretch_len, heads_q * HDIM), kv_total)

    grad_q_all, grad_kv_all = lax.map(backward_seq, jnp.arange(seq_count, dtype=jnp.int32))
    grad_kv_local = lax.psum_scatter(
        grad_kv_all.astype(jnp.bfloat16), "ctx", scatter_dimension=1, tiled=True
    ).astype(jnp.float32)
    grad_keys = (
        rotate(
            grad_kv_local[:, :, :kv_width].reshape(seq_count, stretch_len, heads_kv, HDIM),
            positions,
            -1.0,
        )
        .astype(jnp.bfloat16)
        .reshape(row_count, kv_width)
    )
    grad_values = grad_kv_local[:, :, kv_width:].astype(jnp.bfloat16).reshape(row_count, kv_width)
    grad_queries = (
        rotate(grad_q_all.reshape(seq_count, stretch_len, heads_q, HDIM), positions, -1.0)
        .astype(jnp.bfloat16)
        .reshape(row_count, heads_q * HDIM)
    )
    grad_wquery = tdot(normed1, grad_queries)
    grad_wkey = tdot(normed1, grad_keys)
    grad_wvalue = tdot(normed1, grad_values)
    grad_normed1 = lax.psum(
        (rdot(grad_queries, w_query) + rdot(grad_keys, w_key) + rdot(grad_values, w_value)).astype(
            jnp.bfloat16
        ),
        "tensor",
    ).astype(jnp.float32)
    scaled_one = grad_normed1 * norm1_gain
    grad_gain_one = jnp.sum(grad_normed1 * inputs * inv_one, axis=0)
    grad_in = (
        grad_hidden
        + inv_one * scaled_one
        - inputs
        * (inv_one * inv_one * inv_one)
        * jnp.mean(scaled_one * inputs, axis=1, keepdims=True)
    ).astype(jnp.bfloat16)
    grad_in = grad_in.reshape(seq_count, stretch_len, width_all)
    (
        grad_gain_one,
        grad_wquery,
        grad_wkey,
        grad_wvalue,
        grad_wout,
        grad_gain_two,
        grad_wgate,
        grad_wup,
        grad_wdown,
    ) = (
        lax.psum(grad_gain_one.astype(jnp.bfloat16), ("dp", "ctx")).astype(jnp.float32),
        lax.psum(grad_wquery.astype(jnp.bfloat16), ("dp", "ctx")).astype(jnp.float32),
        lax.psum(grad_wkey.astype(jnp.bfloat16), ("dp", "ctx")).astype(jnp.float32),
        lax.psum(grad_wvalue.astype(jnp.bfloat16), ("dp", "ctx")).astype(jnp.float32),
        lax.psum(grad_wout.astype(jnp.bfloat16), ("dp", "ctx")).astype(jnp.float32),
        lax.psum(grad_gain_two.astype(jnp.bfloat16), ("dp", "ctx")).astype(jnp.float32),
        lax.psum(grad_wgate.astype(jnp.bfloat16), ("dp", "ctx")).astype(jnp.float32),
        lax.psum(grad_wup.astype(jnp.bfloat16), ("dp", "ctx")).astype(jnp.float32),
        lax.psum(grad_wdown.astype(jnp.bfloat16), ("dp", "ctx")).astype(jnp.float32),
    )
    return (
        block_output,
        grad_in,
        grad_gain_one,
        grad_wquery,
        grad_wkey,
        grad_wvalue,
        grad_wout,
        grad_gain_two,
        grad_wgate,
        grad_wup,
        grad_wdown,
    )


def solution(mesh):
    placed = (
        P("dp", "ctx", None),
        P("dp", None),
        P("dp", "ctx"),
        P("dp", "ctx", None),
        P(),
        P(None, "tensor"),
        P(None, "tensor"),
        P(None, "tensor"),
        P("tensor", None),
        P(),
        P(None, "tensor"),
        P(None, "tensor"),
        P("tensor", None),
    )
    return jax.shard_map(
        shards,
        mesh=mesh,
        in_specs=placed,
        out_specs=(
            P("dp", "ctx", None),
            P("dp", "ctx", None),
            P(),
            P(None, "tensor"),
            P(None, "tensor"),
            P(None, "tensor"),
            P("tensor", None),
            P(),
            P(None, "tensor"),
            P(None, "tensor"),
            P("tensor", None),
        ),
        check_vma=False,
    )
```

profile of v0, /device:TPU:0, one launch (start us, length us, event | category | flops | bytes accessed | tf_op | source)
XLA Modules:
  0.0 1100.4 jit_solution(7658305326652356975)
XLA Ops:
  7.8 0.7 convert_element_type.249
  8.5 1.8 fusion.23
  10.9 1.6 copy.31
  12.5 2.8 fusion.60
  15.3 0.9 fusion.54
  16.2 1.1 broadcast_multiply_fusion
  17.5 0.9 pad_maximum_fusion.1
  18.7 4.3 copy.32
  23.0 3.6 fusion.51
  26.6 1.2 subtract_convert_fusion
  27.8 0.9 fusion.5
  28.7 56.0 %all-gather.2.cloned.1.call-done = bf16[1,2048,768]{1,2,0:T(8,128)(2,1)} async-done(((bf16[1,512,768]{1,2,0:T(8,128)(2,1)}), bf16[1,2048,768]{1,2,0:T(8,128)(2,1)}) %all-gather.2.cloned.1.call-update) | async-done | bytes 3145744 | tf_op jit(solution)/shard_map/all_gather | solution.py:103
  84.7 2.2 fusion.75
  87.0 13.8 %fusion.3 = (f32[4,2,512]{2,1,0:T(2,128)S(1)}, f32[4,2048,512,2]{2,1,3,0:T(8,128)}) fusion(pred[512,2048]{0,1:T(8,128)(4,1)S(1)} %fusion.5, bf16[2048,4,96,1]{0,2,3,1:T(8,128)(2,1)S(1)} %bitcast.198, bf16[512,4,2,48]{0,3,2,1:T(8,128)(2,1)S(1)} %bitcast.221, bf16[512,4,2,48]{0,3,2,1:T(8,128)(2,1)S(1)} %bitcast.219), kind=kOutput, calls=%fused_computation.7 | convolution fusion | flops 1637347328 | bytes 36978688 | tf_op jit(solution)/shard_map/while/body/eval_jaxpr/qkgd,skd->kgqs/dot_general | solution.py:43
  100.8 14.4 %exponential_reduce_fusion = f32[4,2,512]{2,1,0:T(2,128)S(1)} fusion(f32[4,2048,512,2]{2,1,3,0:T(8,128)} %get-tuple-element.140, f32[4,2,512]{2,1,0:T(2,128)S(1)} %get-tuple-element.139, pred[512,2048]{0,1:T(8,128)(4,1)S(1)} %fusion.5), kind=kLoop, calls=%fused_computation.5 | loop fusion | flops 33550336 | bytes 34635776 | tf_op jit(solution)/shard_map/while/body/eval_jaxpr/reduce_sum | solution.py:119
  115.2 15.0 %convolution_convert_fusion.10 = bf16[4,96,2,512]{3,1,2,0:T(8,128)(2,1)S(1)} fusion(bf16[2048,4,96,1]{0,2,3,1:T(8,128)(2,1)S(1)} %bitcast.215, f32[4,2048,512,2]{2,1,3,0:T(8,128)} %get-tuple-element.140, f32[4,2,512]{2,1,0:T(2,128)S(1)} %bitcast.230, pred[512,2048]{0,1:T(8,128)(4,1)S(1)} %fusion.5), kind=kOutput, calls=%fused_computation.87 | convolution fusion | flops 1644560384 | bytes 36978688 | tf_op jit(solution)/shard_map/while/body/eval_jaxpr/kgqs,skd->qkgd/dot_general | solution.py:121
  130.2 0.9 copy-done.14
  131.1 2.6 convolution_convert_fusion.6
  134.1 18.7 %all-reduce.8.cloned.1.call-done = bf16[512,1536]{1,0:T(8,128)(2,1)} async-done(((bf16[512,1536]{1,0:T(8,128)(2,1)}), bf16[512,1536]{1,0:T(8,128)(2,1)}) %all-reduce.8.cloned.1.call-update) | async-done | bytes 1572880 | tf_op jit(solution)/shard_map/psum | solution.py:131
  152.8 2.6 multiply_reduce_fusion
  156.3 6.5 fusion.77
  162.8 4.9 fusion.76
  167.8 10.1 multiply_convert_fusion
  177.9 5.2 fusion.78
  183.1 7.6 fusion.34
  190.9 21.5 %all-reduce.10.cloned.1.call-done = bf16[512,1536]{1,0:T(8,128)(2,1)} async-done(((bf16[512,1536]{1,0:T(8,128)(2,1)}), bf16[512,1536]{1,0:T(8,128)(2,1)}) %all-reduce.10.cloned.1.call-update) | async-done | bytes 1572880 | tf_op jit(solution)/shard_map/psum | solution.py:157
  212.4 3.7 fusion.22
  216.2 2.6 fusion.19
  218.8 1.7 copy-done.8
  220.5 2.3 convolution_convert_fusion.9
  222.8 1.4 copy.34
  224.2 1.4 multiply_reduce_fusion.1
  225.6 15.2 %bitcast_convert_fusion = bf16[4,96,2048]{2,1,0:T(8,128)(2,1)} fusion(bf16[512,4,2,96]{0,3,2,1:T(8,128)(2,1)S(1)} %bitcast.210, f32[4,2048,512,2]{2,1,3,0:T(8,128)} %get-tuple-element.140, f32[4,2,512]{2,1,0:T(2,128)S(1)} %bitcast.231, pred[512,2048]{0,1:T(8,128)(4,1)S(1)} %fusion.5), kind=kOutput, calls=%fused_computation.55 | convolution fusion | flops 1644953600 | bytes 36978688 | tf_op jit(solution)/shard_map/while/body/eval_jaxpr/while/body/eval_jaxpr/kgqs,qkgd->skd/dot_general | solution.py:215
  240.8 20.1 %fusion.1 = bf16[4,2,512,2048]{2,3,1,0:T(8,128)(2,1)} fusion(f32[4,2048,512,2]{2,1,3,0:T(8,128)} %get-tuple-element.140, bf16[2048,4,96,1]{0,2,3,1:T(8,128)(2,1)S(1)} %bitcast.216, bf16[512,4,2,96]{0,3,2,1:T(8,128)(2,1)S(1)} %bitcast.211, f32[4,2,512]{2,1,0:T(2,128)S(1)} %bitcast.229, f32[4,2,512]{2,1,0:T(2,128)S(1)} %bitcast.232, ...), kind=kOutput, calls=%fused_computation.2 | convolution fusion | flops 1660944384 | bytes 53772288 | tf_op jit(solution)/shard_map/while/body/eval_jaxpr/while/body/eval_jaxpr/qkgd,skd->kgqs/dot_general | solution.py:199
  260.9 11.2 %fusion.32 = bf16[4,96,2048]{2,1,0:T(8,128)(2,1)S(1)} fusion(bf16[4,2,512,2048]{2,3,1,0:T(8,128)(2,1)} %fusion.1, bf16[512,4,2,48]{0,3,2,1:T(8,128)(2,1)} %bitcast.220, bf16[512,4,2,48]{0,3,2,1:T(8,128)(2,1)} %bitcast.218), kind=kOutput, calls=%fused_computation.57 | convolution fusion | flops 1613758464 | bytes 19136512 | tf_op jit(solution)/shard_map/while/body/eval_jaxpr/while/body/eval_jaxpr/kgqs,qkgd->skd/dot_general | solution.py:210
  272.1 3.5 pad_maximum_fusion
  275.9 8.1 convolution_convert_fusion.5
  284.0 8.5 convolution_multiply_fusion
  292.9 0.9 copy-done.33
  293.8 0.7 copy-done.19
  294.5 3.1 fusion.79
  297.6 39.8 %reduce-scatter.2.cloned.1.call-done = bf16[1,512,768]{1,2,0:T(8,128)(2,1)} async-done(((bf16[1,2048,768]{1,2,0:T(8,128)(2,1)}), bf16[1,512,768]{1,2,0:T(8,128)(2,1)}) %reduce-scatter.2.cloned.1.call-update) | async-done | bytes 786448 | tf_op jit(solution)/shard_map/reduce_scatter | solution.py:231
  337.4 1.0 slice.66
  338.7 3.1 convolution_add_fusion.1
  341.8 2.2 fusion.33
  344.3 1.1 copy-done.21
  345.4 7.1 convolution_convert_fusion.1
  352.5 5.3 convolution_convert_fusion.2
  357.9 5.4 convolution_convert_fusion
  363.3 3.0 convolution_convert_fusion.4
  366.3 2.8 convolution_convert_fusion.3
  369.2 2.2 convolution_convert_fusion.8
  371.4 2.2 convolution_convert_fusion.7
  373.6 2.6 fusion.29
  376.2 45.2 %all-reduce = (bf16[1536]{0:T(1024)(128)(2,1)S(1)}, bf16[1536]{0:T(1024)(128)(2,1)S(1)}) all-reduce(bf16[1536]{0:T(1024)(128)(2,1)S(1)} %get-tuple-element.94, bf16[1536]{0:T(1024)(128)(2,1)S(1)} %get-tuple-element.92), channel_id=1, replica_groups=mesh['dp'=4,'ctx'=4,'tensor'=2] {'dp','ctx'}, use_global_device_ids=true, to_apply=%region_13.14 | all-reduce | flops 3072 | bytes 12288 | tf_op jit(solution)/shard_map/psum | solution.py:279
  422.6 5.6 fusion.38
  428.1 632.3 %all-reduce.12.cloned.1.call-done = (bf16[1536,768]{1,0:T(8,128)(2,1)}, bf16[1536,384]{1,0:T(8,128)(2,1)}, bf16[1536,384]{1,0:T(8,128)(2,1)}, bf16[768,1536]{1,0...) async-done(((bf16[1536,768]{1,0:T(8,128)(2,1)}, bf16[1536,384]{1,0:T(8,128)(2,1)}, bf16[1536,384]{1,0:T(8,128)(2,1)}, ...) | async-done | bytes 25952272 | tf_op jit(solution)/shard_map/psum | solution.py:280
  1060.4 4.3 convert_element_type.284
  1064.7 1.6 convert_element_type.286
  1066.5 1.6 convert_element_type.288
  1068.0 2.9 convert_element_type.290
  1071.0 9.2 convert_element_type.294
  1080.2 6.3 convert_element_type.296
  1086.5 6.6 convert_element_type.298
  (133 shorter events, 5.9 us)
Async XLA Ops:
  7.2 123.9 %copy-start = (bf16[768,1536]{1,0:T(8,128)(2,1)S(1)}, bf16[768,1536]{1,0:T(8,128)(2,1)}, u32[]{:S(2)}) copy-start(bf16[768,1536]{1,0:T(8,128)(2,1)} %param.21) | copy-start | bytes 7077892
  7.2 5.3 copy-start.36
  7.2 77.5 %all-gather.2.cloned.1.call-start = ((), (), s32[]{:S(2)}) async-start(), calls=%async_computation.1 | async-start | bytes 3932160 | tf_op jit(solution)/shard_map/all_gather | solution.py:103
  10.9 12.1 %copy-start.38 = (f32[512]{0:T(512)}, f32[512]{0:T(512)S(1)}, u32[]{:S(2)}) copy-start(f32[512]{0:T(512)S(1)} %get-tuple-element.136) | copy-start | bytes 6148
  12.5 2.8 copy-start.2
  15.3 0.9 copy-start.42
  17.3 9.3 copy-start.16
  18.4 4.6 copy-start.40
  18.4 134.4 %all-reduce.8.cloned.1.call-start = ((), (), s32[]{:S(2)}) async-start(), calls=%async_computation.2 | async-start | bytes 3145728 | tf_op jit(solution)/shard_map/psum | solution.py:131
  84.7 2.2 copy-start.26
  84.7 2.2 copy-start.27
  86.9 13.8 %copy-start.10 = (bf16[2048,384]{0,1:T(8,128)(2,1)}, bf16[2048,384]{0,1:T(8,128)(2,1)S(1)}, u32[]{:S(2)}) copy-start(bf16[2048,384]{0,1:T(8,128)(2,1)S(1)} %get-tuple-element.120) | copy-start | bytes 4718596
  86.9 28.3 %copy-start.22 = (bf16[2048,384]{0,1:T(8,128)(2,1)}, bf16[2048,384]{0,1:T(8,128)(2,1)S(1)}, u32[]{:S(2)}) copy-start(bf16[2048,384]{0,1:T(8,128)(2,1)S(1)} %get-tuple-element.121) | copy-start | bytes 4718596
  130.2 0.9 copy-start.14
  133.6 21.8 %copy-start.35 = (f32[1536]{0:T(1024)S(1)}, f32[1536]{0:T(1024)}, u32[]{:S(2)}) copy-start(f32[1536]{0:T(1024)} %param.22) | copy-start | bytes 18436
  133.7 78.8 %all-reduce.10.cloned.1.call-start = ((), (), s32[]{:S(2)}) async-start(), calls=%async_computation.3 | async-start | bytes 3145728 | tf_op jit(solution)/shard_map/psum | solution.py:157
  152.8 2.6 copy-start.3
  152.8 2.8 copy-start.6
  155.7 7.1 slice-start.4
  156.2 6.5 copy-start.20
  156.3 6.5 slice-start.5
  162.8 4.9 copy-start.24
  177.9 5.2 copy-start.44
  190.7 146.7 %reduce-scatter.2.cloned.1.call-start = ((), (), s32[]{:S(2)}) async-start(), calls=%async_computation.4 | async-start | bytes 3932160 | tf_op jit(solution)/shard_map/reduce_scatter | solution.py:231
  212.4 3.7 copy-start.4
  212.4 3.7 copy-start.7
  212.4 3.8 copy-start.12
  218.8 1.7 copy-start.8
  225.6 15.3 %copy-start.23 = (bf16[2048,384]{0,1:T(8,128)(2,1)S(1)}, bf16[2048,384]{0,1:T(8,128)(2,1)}, u32[]{:S(2)}) copy-start(bf16[2048,384]{0,1:T(8,128)(2,1)} %copy-done.22) | copy-start | bytes 4718596
  275.6 98.0 %all-reduce.14.cloned.1.call-start = ((), (), s32[]{:S(2)}) async-start(), calls=%async_computation.6 | async-start | bytes 6291456 | tf_op jit(solution)/shard_map/psum | solution.py:142
  275.9 8.1 copy-start.11
  284.0 8.5 copy-start.17
  284.0 8.5 copy-start.31
  292.5 2.0 copy-start.19
  292.9 0.9 copy-start.33
  297.6 41.1 %copy-start.13 = (bf16[1536,384]{1,0:T(8,128)(2,1)S(1)}, bf16[1536,384]{1,0:T(8,128)(2,1)}, u32[]{:S(2)}) copy-start(bf16[1536,384]{1,0:T(8,128)(2,1)} %param.19) | copy-start | bytes 3538948
  338.7 3.1 copy-start.30
  338.7 3.1 copy-start.32
  344.0 1.4 copy-start.21
  344.0 716.4 %all-reduce.12.cloned.1.call-start = ((), (), s32[]{:S(2)}) async-start(), calls=%async_computation.5 | async-start | bytes 51904512 | tf_op jit(solution)/shard_map/psum | solution.py:280
  345.4 7.1 copy-start.43
  352.5 5.4 copy-start.25
  352.5 5.4 copy-start.45
  357.9 5.4 copy-start.5
  357.9 5.4 copy-start.34
  357.9 5.4 copy-start.37
  357.9 5.4 copy-start.39
  363.3 3.0 copy-start.9
  363.3 3.0 copy-start.15
  373.6 49.0 %copy-start.41 = (f32[512]{0:T(512)S(1)}, f32[512]{0:T(512)}, u32[]{:S(2)}) copy-start(f32[512]{0:T(512)} %get-tuple-element.135) | copy-start | bytes 6148
  1060.4 4.3 copy-start.29
  1064.7 1.7 copy-start.28
  1064.7 3.3 copy-start.18
  1068.0 12.2 %slice-start.2 = ((s8[6291456]{0:T(1024)(128)(4,1)}), s8[4194304]{0:T(1024)(128)(4,1)S(1)}, s32[]{:S(2)}) async-start(s8[6291456]{0:T(1024)(128)(4,1)} %bitcast.204), calls=%async_computation.9 | async-start | bytes 8388608
  1071.0 9.3 slice-start.3
  1071.0 15.6 %slice-start = ((s8[6291456]{0:T(1024)(128)(4,1)}), s8[4194304]{0:T(1024)(128)(4,1)S(1)}, s32[]{:S(2)}) async-start(s8[6291456]{0:T(1024)(128)(4,1)} %bitcast.202), calls=%async_computation.7 | async-start | bytes 8388608
  1080.2 6.3 slice-start.1
  1086.5 6.6 copy-start.1
Sparse Core Ops, SparseCore 0:
  18.5 66.1 all-gather.1
  133.8 18.9 all-reduce.7
  190.8 21.5 all-reduce.9
  275.8 61.5 reduce-scatter.1
  344.1 23.2 all-reduce.13
  374.9 685.5 all-reduce.11
where the time goes:
time: 1100 us
  waiting for transfers between devices  768 us (70%)
  matrix products  175 us (16%)
  other arithmetic  79.1 us (7%)
  blocking collectives  45.2 us (4%)
  local copies, waits for them, and re-layouts  16.3 us (1%)
  between operations  15.2 us (1%)
    psum x1, waiting for transfers between devices, shards(): lax.psum(grad_wquery.astype(jnp.bfloat16), ('dp', 'ctx'))  632 us
    all_gather x1, waiting for transfers between devices, shards(): whole_kv = lax.all_gather(local_kv, 'ctx', axis=1, tiled=True)  56 us
    psum x1, blocking collectives, shards(): lax.psum(grad_gain_one.astype(jnp.bfloat16), ('dp', 'ctx'))  45.2 us
    reduce_scatter x1, waiting for transfers between devices, shards(): lax.psum_scatter(grad_kv_all.astype(jnp.bfloat16), 'ctx', scatter_dimensi...  39.8 us
    dot_general x7, matrix products, rdot(): lax.dot_general(left, right, (((1,), (1,)), ((), ())), preferred_element_...  33.6 us
    dot_general x7, matrix products, tdot(): lax.dot_general(left, right, (((0,), (0,)), ((), ())), preferred_element_...  28 us
  transfers between devices with their start and end apart: 6, of which 5 were waited for; matrix products, arithmetic and copies ran while one was open for 6% of the time, Pallas kernels for 0%

commit v1 on v0

--- a/solution.py
+++ b/solution.py
@@ -277,7 +277,9 @@
         grad_wdown,
     ) = (
         lax.psum(grad_gain_one.astype(jnp.bfloat16), ("dp", "ctx")).astype(jnp.float32),
-        lax.psum(grad_wquery.astype(jnp.bfloat16), ("dp", "ctx")).astype(jnp.float32),
+        jnp.sum(lax.all_gather(grad_wquery.astype(jnp.bfloat16), ("dp", "ctx")), axis=0).astype(
+            jnp.float32
+        ),
         lax.psum(grad_wkey.astype(jnp.bfloat16), ("dp", "ctx")).astype(jnp.float32),
         lax.psum(grad_wvalue.astype(jnp.bfloat16), ("dp", "ctx")).astype(jnp.float32),
         lax.psum(grad_wout.astype(jnp.bfloat16), ("dp", "ctx")).astype(jnp.float32),

time: 1100 us -> 1420 us (1.29)
  waiting for transfers between devices: 768 us -> 1070 us
  other arithmetic: 79.1 us -> 95.6 us
    all_gather x0 -> x1, waiting for transfers between devices: none -> 362 us  [shards(): lax.all_gather(grad_wquery.astype(jnp.bfloat16), ('dp', 'ctx'))]
    psum x1, waiting for transfers between devices: 632 us -> 568 us  [shards(): lax.psum(grad_wkey.astype(jnp.bfloat16), ('dp', 'ctx')).astype(jnp.float32)]
    reduce_sum x0 -> x1, other arithmetic: none -> 14.8 us  [shards(): jnp.sum(lax.all_gather(grad_wquery.astype(jnp.bfloat16), ('dp', 'ctx')),...]
  transfers between devices with their start and end apart: 6 -> 7, of which waited for: 5 -> 6; matrix products, arithmetic and copies ran while one was open for 6% -> 7% of each run, Pallas kernels for 0% -> 0%
where the time goes in v1:
time: 1420 us
  waiting for transfers between devices  1070 us (75%)
  matrix products  175 us (12%)
  other arithmetic  95.6 us (7%)
  blocking collectives  45.3 us (3%)
  local copies, waits for them, and re-layouts  17 us (1%)
  between operations  14.9 us (1%)
    psum x1, waiting for transfers between devices, shards(): lax.psum(grad_wkey.astype(jnp.bfloat16), ('dp', 'ctx')).astype(jnp.float32)  568 us
    all_gather x1, waiting for transfers between devices, shards(): lax.all_gather(grad_wquery.astype(jnp.bfloat16), ('dp', 'ctx'))  362 us
    all_gather x1, waiting for transfers between devices, shards(): whole_kv = lax.all_gather(local_kv, 'ctx', axis=1, tiled=True)  56 us
    psum x1, blocking collectives, shards(): lax.psum(grad_gain_one.astype(jnp.bfloat16), ('dp', 'ctx'))  45.3 us
    reduce_scatter x1, waiting for transfers between devices, shards(): lax.psum_scatter(grad_kv_all.astype(jnp.bfloat16), 'ctx', scatter_dimensi...  39.8 us
    dot_general x7, matrix products, rdot(): lax.dot_general(left, right, (((1,), (1,)), ((), ())), preferred_element_...  33.6 us
  transfers between devices with their start and end apart: 7, of which 6 were waited for; matrix products, arithmetic and copies ran while one was open for 7% of the time, Pallas kernels for 0%

profile of v1, /device:TPU:0, one launch (start us, length us, event | category | flops | bytes accessed | tf_op | source)
XLA Modules:
  0.0 1415.3 jit_solution(16786642829205806621)
XLA Ops:
  8.5 1.8 fusion.23
  10.9 1.6 copy.31
  12.5 2.8 fusion.60
  15.3 0.9 fusion.54
  16.2 1.1 broadcast_multiply_fusion
  17.5 0.9 pad_maximum_fusion.1
  18.8 4.3 copy.32
  23.1 3.6 fusion.51
  26.7 1.1 subtract_convert_fusion
  27.9 0.9 fusion.5
  28.8 56.0 %all-gather.4.cloned.1.call-done = bf16[1,2048,768]{1,2,0:T(8,128)(2,1)} async-done(((bf16[1,512,768]{1,2,0:T(8,128)(2,1)}), bf16[1,2048,768]{1,2,0:T(8,128)(2,1)}) %all-gather.4.cloned.1.call-update) | async-done | bytes 3145744 | tf_op jit(solution)/shard_map/all_gather | solution.py:103
  84.8 2.2 fusion.75
  87.0 13.8 fusion.3
  100.8 14.4 %exponential_reduce_fusion = f32[4,2,512]{2,1,0:T(2,128)S(1)} fusion(f32[4,2048,512,2]{2,1,3,0:T(8,128)} %get-tuple-element.139, f32[4,2,512]{2,1,0:T(2,128)S(1)} %get-tuple-element.138, pred[512,2048]{0,1:T(8,128)(4,1)S(1)} %fusion.5), kind=kLoop, calls=%fused_computation.5 | loop fusion | flops 33550336 | bytes 34635776 | tf_op jit(solution)/shard_map/while/body/eval_jaxpr/reduce_sum | solution.py:119
  115.2 15.0 %convolution_convert_fusion.10 = bf16[4,96,2,512]{3,1,2,0:T(8,128)(2,1)S(1)} fusion(bf16[2048,4,96,1]{0,2,3,1:T(8,128)(2,1)S(1)} %bitcast.217, f32[4,2048,512,2]{2,1,3,0:T(8,128)} %get-tuple-element.139, f32[4,2,512]{2,1,0:T(2,128)S(1)} %bitcast.232, pred[512,2048]{0,1:T(8,128)(4,1)S(1)} %fusion.5), kind=kOutput, calls=%fused_computation.87 | convolution fusion | flops 1644560384 | bytes 36978688 | tf_op jit(solution)/shard_map/while/body/eval_jaxpr/kgqs,skd->qkgd/dot_general | solution.py:121
  130.2 0.9 copy-done.14
  131.1 2.6 convolution_convert_fusion.6
  134.3 18.6 %all-reduce.8.cloned.1.call-done = bf16[512,1536]{1,0:T(8,128)(2,1)} async-done(((bf16[512,1536]{1,0:T(8,128)(2,1)}), bf16[512,1536]{1,0:T(8,128)(2,1)}) %all-reduce.8.cloned.1.call-update) | async-done | bytes 1572880 | tf_op jit(solution)/shard_map/psum | solution.py:131
  152.9 2.6 multiply_reduce_fusion
  156.3 6.5 fusion.77
  162.9 4.9 fusion.76
  167.8 10.1 multiply_convert_fusion
  177.9 5.2 fusion.78
  183.2 7.6 fusion.34
  191.0 21.5 %all-reduce.10.cloned.1.call-done = bf16[512,1536]{1,0:T(8,128)(2,1)} async-done(((bf16[512,1536]{1,0:T(8,128)(2,1)}), bf16[512,1536]{1,0:T(8,128)(2,1)}) %all-reduce.10.cloned.1.call-update) | async-done | bytes 1572880 | tf_op jit(solution)/shard_map/psum | solution.py:157
  212.5 3.7 fusion.22
  216.3 2.6 fusion.19
  218.9 1.7 copy-done.8
  220.5 2.3 convolution_convert_fusion.9
  222.9 1.4 copy.34
  224.3 1.4 multiply_reduce_fusion.1
  225.7 15.2 %bitcast_convert_fusion = bf16[4,96,2048]{2,1,0:T(8,128)(2,1)} fusion(bf16[512,4,2,96]{0,3,2,1:T(8,128)(2,1)S(1)} %bitcast.212, f32[4,2048,512,2]{2,1,3,0:T(8,128)} %get-tuple-element.139, f32[4,2,512]{2,1,0:T(2,128)S(1)} %bitcast.233, pred[512,2048]{0,1:T(8,128)(4,1)S(1)} %fusion.5), kind=kOutput, calls=%fused_computation.55 | convolution fusion | flops 1644953600 | bytes 36978688 | tf_op jit(solution)/shard_map/while/body/eval_jaxpr/while/body/eval_jaxpr/kgqs,qkgd->skd/dot_general | solution.py:215
  240.9 20.1 %fusion.1 = bf16[4,2,512,2048]{2,3,1,0:T(8,128)(2,1)} fusion(f32[4,2048,512,2]{2,1,3,0:T(8,128)} %get-tuple-element.139, bf16[2048,4,96,1]{0,2,3,1:T(8,128)(2,1)S(1)} %bitcast.218, bf16[512,4,2,96]{0,3,2,1:T(8,128)(2,1)S(1)} %bitcast.213, f32[4,2,512]{2,1,0:T(2,128)S(1)} %bitcast.231, f32[4,2,512]{2,1,0:T(2,128)S(1)} %bitcast.234, ...), kind=kOutput, calls=%fused_computation.2 | convolution fusion | flops 1660944384 | bytes 53772288 | tf_op jit(solution)/shard_map/while/body/eval_jaxpr/while/body/eval_jaxpr/qkgd,skd->kgqs/dot_general | solution.py:199
  261.0 11.2 fusion.32
  272.2 3.5 pad_maximum_fusion
  276.0 8.1 convolution_convert_fusion.5
  284.1 8.5 convolution_multiply_fusion
  294.6 3.1 fusion.79
  297.7 39.8 %reduce-scatter.2.cloned.1.call-done = bf16[1,512,768]{1,2,0:T(8,128)(2,1)} async-done(((bf16[1,2048,768]{1,2,0:T(8,128)(2,1)}), bf16[1,512,768]{1,2,0:T(8,128)(2,1)}) %reduce-scatter.2.cloned.1.call-update) | async-done | bytes 786448 | tf_op jit(solution)/shard_map/reduce_scatter | solution.py:231
  337.5 1.0 slice.66
  338.8 3.1 convolution_add_fusion.1
  341.9 2.2 fusion.33
  344.6 0.9 copy-done.21
  345.5 7.1 convolution_convert_fusion.1
  352.6 5.3 convolution_convert_fusion.2
  358.0 5.4 convolution_convert_fusion
  363.4 2.8 convolution_convert_fusion.3
  366.2 2.2 convolution_convert_fusion.8
  368.4 2.2 convolution_convert_fusion.7
  370.6 1.1 copy-done.33
  371.7 3.0 convolution_convert_fusion.4
  374.7 2.6 fusion.29
  377.3 45.3 %all-reduce = (bf16[1536]{0:T(1024)(128)(2,1)S(1)}, bf16[1536]{0:T(1024)(128)(2,1)S(1)}) all-reduce(bf16[1536]{0:T(1024)(128)(2,1)S(1)} %get-tuple-element.94, bf16[1536]{0:T(1024)(128)(2,1)S(1)} %get-tuple-element.92), channel_id=1, replica_groups=mesh['dp'=4,'ctx'=4,'tensor'=2] {'dp','ctx'}, use_global_device_ids=true, to_apply=%region_13.14 | all-reduce | flops 3072 | bytes 12288 | tf_op jit(solution)/shard_map/psum | solution.py:279
  423.8 5.2 fusion.38
  429.1 567.7 %all-reduce.12.cloned.1.call-done = (bf16[1536,384]{1,0:T(8,128)(2,1)}, bf16[1536,384]{1,0:T(8,128)(2,1)}, bf16[768,1536]{1,0:T(8,128)(2,1)}, bf16[1536,2048]{1,...) async-done(((bf16[1536,384]{1,0:T(8,128)(2,1)}, bf16[1536,384]{1,0:T(8,128)(2,1)}, bf16[768,1536]{1,0:T(8,128)(2,1)}, bf16[1536,2048]{1,0:T(8,128)(2,1)}, ...) | async-done | bytes 23592976 | tf_op jit(solution)/shard_map/psum | solution.py:283
  996.8 3.0 convert_element_type.288
  999.7 1.6 convert_element_type.290
  1001.3 2.9 convert_element_type.292
  1004.2 10.0 convert_element_type.296
  1014.2 6.3 convert_element_type.298
  1020.5 6.6 convert_element_type.300
  1027.1 362.2 %all-gather.6.cloned.1.call-done = bf16[24576,768]{1,0:T(8,128)(2,1)} async-done(((bf16[1536,768]{1,0:T(8,128)(2,1)}), bf16[24576,768]{1,0:T(8,128)(2,1)}) %all-gather.6.cloned.1.call-update) | async-done | bytes 37748752 | tf_op jit(solution)/shard_map/all_gather | solution.py:280
  1389.3 14.8 %reduce_sum.94 = bf16[1536,768]{1,0:T(8,128)(2,1)} reduce(bf16[16,1536,768]{2,1,0:T(8,128)(2,1)} %bitcast.199, bf16[]{:T(256)} %constant.163.clone.1), dimensions={0}, to_apply=%region_14.15 | reduce | flops 17694720 | bytes 40108032 | tf_op jit(solution)/shard_map/reduce_sum | solution.py:280
  1404.1 4.2 convert_element_type.286
  (135 shorter events, 8.5 us)
Async XLA Ops:
  7.2 124.0 %copy-start = (bf16[768,1536]{1,0:T(8,128)(2,1)S(1)}, bf16[768,1536]{1,0:T(8,128)(2,1)}, u32[]{:S(2)}) copy-start(bf16[768,1536]{1,0:T(8,128)(2,1)} %param.21) | copy-start | bytes 7077892
  7.2 5.3 copy-start.35
  7.2 77.6 %all-gather.4.cloned.1.call-start = ((), (), s32[]{:S(2)}) async-start(), calls=%async_computation.1 | async-start | bytes 3932160 | tf_op jit(solution)/shard_map/all_gather | solution.py:103
  10.9 12.2 copy-start.37
  12.5 2.8 copy-start.2
  15.3 0.9 copy-start.41
  17.3 9.4 copy-start.16
  18.4 4.7 copy-start.39
  18.4 134.4 %all-reduce.8.cloned.1.call-start = ((), (), s32[]{:S(2)}) async-start(), calls=%async_computation.2 | async-start | bytes 3145728 | tf_op jit(solution)/shard_map/psum | solution.py:131
  84.8 2.2 copy-start.26
  84.8 2.2 copy-start.27
  87.0 13.8 copy-start.10
  87.0 28.2 %copy-start.22 = (bf16[2048,384]{0,1:T(8,128)(2,1)}, bf16[2048,384]{0,1:T(8,128)(2,1)S(1)}, u32[]{:S(2)}) copy-start(bf16[2048,384]{0,1:T(8,128)(2,1)S(1)} %get-tuple-element.120) | copy-start | bytes 4718596
  130.2 0.9 copy-start.14
  133.7 21.8 %copy-start.34 = (f32[1536]{0:T(1024)S(1)}, f32[1536]{0:T(1024)}, u32[]{:S(2)}) copy-start(f32[1536]{0:T(1024)} %param.22) | copy-start | bytes 18436
  133.7 78.8 %all-reduce.10.cloned.1.call-start = ((), (), s32[]{:S(2)}) async-start(), calls=%async_computation.3 | async-start | bytes 3145728 | tf_op jit(solution)/shard_map/psum | solution.py:157
  152.9 2.6 copy-start.3
  152.9 2.8 copy-start.6
  155.7 7.1 slice-start.4
  156.3 6.5 copy-start.20
  156.3 6.5 slice-start.5
  162.9 4.9 copy-start.24
  177.9 5.2 copy-start.43
  190.8 146.7 %reduce-scatter.2.cloned.1.call-start = ((), (), s32[]{:S(2)}) async-start(), calls=%async_computation.4 | async-start | bytes 3932160 | tf_op jit(solution)/shard_map/reduce_scatter | solution.py:231
  212.5 3.7 copy-start.4
  212.5 3.7 copy-start.7
  212.5 3.8 copy-start.12
  218.9 1.7 copy-start.8
  225.7 15.3 %copy-start.23 = (bf16[2048,384]{0,1:T(8,128)(2,1)S(1)}, bf16[2048,384]{0,1:T(8,128)(2,1)}, u32[]{:S(2)}) copy-start(bf16[2048,384]{0,1:T(8,128)(2,1)} %copy-done.22) | copy-start | bytes 4718596
  275.7 99.0 %all-reduce.14.cloned.1.call-start = ((), (), s32[]{:S(2)}) async-start(), calls=%async_computation.7 | async-start | bytes 6291456 | tf_op jit(solution)/shard_map/psum | solution.py:142
  276.0 8.1 copy-start.11
  284.1 8.5 copy-start.17
  284.1 8.5 copy-start.30
  292.6 2.0 copy-start.19
  293.0 0.9 copy-start.32
  297.7 41.1 %copy-start.13 = (bf16[1536,384]{1,0:T(8,128)(2,1)S(1)}, bf16[1536,384]{1,0:T(8,128)(2,1)}, u32[]{:S(2)}) copy-start(bf16[1536,384]{1,0:T(8,128)(2,1)} %param.19) | copy-start | bytes 3538948
  338.8 3.1 copy-start.29
  338.8 3.1 copy-start.31
  344.1 1.4 copy-start.21
  344.1 652.6 %all-reduce.12.cloned.1.call-start = ((), (), s32[]{:S(2)}) async-start(), calls=%async_computation.6 | async-start | bytes 47185920 | tf_op jit(solution)/shard_map/psum | solution.py:283
  345.5 7.1 copy-start.42
  352.6 5.4 copy-start.25
  352.6 5.4 copy-start.44
  358.0 5.4 copy-start.9
  358.0 5.4 copy-start.15
  363.3 2.8 copy-start.5
  363.3 2.8 copy-start.36
  363.3 2.8 copy-start.38
  370.6 1.1 copy-start.33
  370.6 1018.7 %all-gather.6.cloned.1.call-start = ((), (), s32[]{:S(2)}) async-start(), calls=%async_computation.5 | async-start | bytes 40108032 | tf_op jit(solution)/shard_map/all_gather | solution.py:280
  374.7 49.2 %copy-start.40 = (f32[512]{0:T(512)S(1)}, f32[512]{0:T(512)}, u32[]{:S(2)}) copy-start(f32[512]{0:T(512)} %get-tuple-element.134) | copy-start | bytes 6148
  996.7 3.0 copy-start.28
  996.8 4.5 copy-start.18
  1001.3 12.9 slice-start.2
  1004.2 10.0 slice-start.3
  1004.2 16.3 %slice-start = ((s8[6291456]{0:T(1024)(128)(4,1)}), s8[4194304]{0:T(1024)(128)(4,1)S(1)}, s32[]{:S(2)}) async-start(s8[6291456]{0:T(1024)(128)(4,1)} %bitcast.204), calls=%async_computation.8 | async-start | bytes 8388608
  1014.2 6.3 slice-start.1
  1389.3 19.0 %copy-start.1 = (bf16[768,1536]{1,0:T(8,128)(2,1)S(1)}, bf16[768,1536]{1,0:T(8,128)(2,1)}, u32[]{:S(2)}) copy-start(bf16[768,1536]{1,0:T(8,128)(2,1)} %param.21) | copy-start | bytes 7077892
Sparse Core Ops, SparseCore 0:
  18.6 66.1 all-gather.3
  133.8 19.0 all-reduce.7
  190.9 21.5 all-reduce.9
  275.8 61.5 reduce-scatter.1
  344.2 23.2 all-reduce.13
  374.9 621.7 all-reduce.11
  1000.1 389.1 all-gather.5
